TPU v7x, 8 devices: a whole 2x2x1 slice. The times are simulated.
8 devices in a mesh: dp: 1 (over z), sp: 8 (over x, y, core).
Axes of the slice: x: 2, y: 2, z: 1, core: 2. Of those that a mesh axis runs over, the one named last changes fastest.
Arguments:
- q: bfloat16 [32, 32, 128], P('dp')
- k: bfloat16 [32, 8192, 4, 128], P('dp', 'sp')
- v: bfloat16 [32, 8192, 4, 128], P('dp', 'sp')
Outputs:
- q: bfloat16 [32, 32, 128], P('dp')
All inputs are finite; a program needn't handle non-finite values.
Results may differ from a plain program's by a relative error of at most 0.012.
Values are sent between devices in bfloat16 or wider.
A program may use at most 2 GiB of HBM per device.

v0:
```python
import jax
import jax.numpy as jnp
from jax import lax
from jax.sharding import PartitionSpec as P


def einsum(form, a, b):
    return jnp.einsum(form, a.astype(jnp.float32), b.astype(jnp.float32))


def part_of(q, k, v):
    grouped = q.reshape(q.shape[0], k.shape[2], -1, q.shape[2])
    scores = einsum("bgsd,bugd->bgsu", grouped, k) * q.shape[2] ** -0.5
    high = jnp.max(scores, -1, keepdims=True)
    weights = jnp.exp(scores - high)
    seen = einsum("bgsu,bugd->bgsd", weights.astype(jnp.bfloat16), v)
    return jnp.concatenate([seen, jnp.sum(weights, -1, keepdims=True), high], -1)


def together(parts):
    seen, total, high = parts[..., :-2], parts[..., -2:-1], parts[..., -1:]
    scale = jnp.exp(high - jnp.max(high, 0))
    return (jnp.sum(seen * scale, 0) / jnp.sum(total * scale, 0)).astype(jnp.bfloat16)


def solution(mesh):
    def step(q, k, v):
        return together(lax.all_gather(part_of(q, k, v), "sp")).reshape(q.shape)

    return jax.shard_map(
        step,
        mesh=mesh,
        in_specs=(P("dp", None, None), P("dp", "sp", None, None), P("dp", "sp", None, None)),
        out_specs=P("dp", None, None),
        check_vma=False,
    )
```

profile of v0, /device:TPU:0, one launch (start us, length us, event | category | flops | bytes accessed | tf_op | source)
XLA Modules:
  0.0 124.3 jit_solution(17035243101802993517)
XLA Ops:
  6.5 0.0 copy-start
  6.5 0.0 all-gather.3.cloned.1.call-start
  6.5 0.9 copy-done
  7.5 16.6 %multiply_reduce_fusion = (f32[32,4,8]{2,1,0:T(4,128)S(1)}, f32[32,4,8,1024]{3,2,1,0:T(8,128)S(1)}) fusion(bf16[32,1024,4,128]{3,2,1,0:T(4,128)(2,1)} %param.4, bf16[32,32,128]{2,1,0:T(8,128)(2,1)S(1)} %copy-done), kind=kOutput, calls=%fused_computation.11 | convolution fusion | flops 270531584 | bytes 38014976 | tf_op jit(solution)/shard_map/bgsd,bugd->bgsu/dot_general | solution.py:8
  24.1 0.0 copy-start.2
  24.1 1.9 %copy-done.2 = f32[32,4,8,1024]{3,2,1,0:T(8,128)} copy-done((f32[32,4,8,1024]{3,2,1,0:T(8,128)}, f32[32,4,8,1024]{3,2,1,0:T(8,128)S(1)}, u32[]{:S(2)}) %copy-start.2) | copy-done | bytes 4194328
  26.1 0.9 fusion.6
  27.0 18.0 %fusion = f32[32,4,8,128]{3,2,1,0:T(8,128)S(1)} fusion(bf16[32,1024,4,128]{3,2,1,0:T(4,128)(2,1)} %param.5, f32[32,4,8,1024]{3,2,1,0:T(8,128)} %copy-done.2, f32[32,4,8]{2,1,0:T(4,128)S(1)} %get-tuple-element.7), kind=kOutput, calls=%fused_computation | convolution fusion | flops 271581184 | bytes 38277120 | tf_op jit(solution)/shard_map/bgsu,bugd->bgsd/dot_general | solution.py:8
  45.0 0.8 copy.35
  45.8 0.8 copy.36
  46.6 1.3 %pad_maximum_fusion = f32[32,4,8,130]{3,2,1,0:T(8,128)} fusion(f32[32,4,8,1]{3,2,1,0:T(8,128)S(1)} %copy.36, f32[32,4,8,1]{3,2,1,0:T(8,128)S(1)} %copy.35, f32[32,4,8,128]{3,2,1,0:T(8,128)S(1)} %fusion), kind=kLoop, calls=%fused_computation.16 | loop fusion | flops 266240 | bytes 1064960 | tf_op jit(solution)/shard_map/concatenate | solution.py:17
  47.9 0.0 all-gather.3.cloned.1.call-update
  47.9 51.3 %all-gather.3.cloned.1.call-done = f32[256,4,8,130]{3,2,1,0:T(8,128)} async-done(((f32[32,4,8,130]{3,2,1,0:T(8,128)}), f32[256,4,8,130]{3,2,1,0:T(8,128)}) %all-gather.3.cloned.1.call-update) | async-done | bytes 4259856 | tf_op jit(solution)/shard_map/all_gather | solution.py:28
  99.3 3.5 %slice_reduce_fusion = f32[32,4,8]{2,1,0:T(4,128)S(1)} fusion(f32[8,32,4,8,130]{4,3,2,1,0:T(8,128)} %bitcast.14), kind=kLoop, calls=%fused_computation.10 | loop fusion | flops 7168 | bytes 36864 | tf_op jit(solution)/shard_map/reduce_max | solution.py:22
  102.8 6.8 %fusion.4 = (f32[32,4,8]{2,1,0:T(4,128)S(1)}, f32[8,32,4,8,1]{4,3,2,1,0:T(8,128)}) fusion(f32[8,32,4,8,130]{4,3,2,1,0:T(8,128)} %bitcast.15, f32[32,4,8]{2,1,0:T(4,128)S(1)} %slice_reduce_fusion), kind=kLoop, calls=%fused_computation.5 | loop fusion | flops 23552 | bytes 106496 | tf_op jit(solution)/shard_map/reduce_sum | solution.py:23
  109.5 0.1 copy.39
  109.6 0.1 copy.40
  109.7 0.0 copy-start.1
  109.7 3.7 %copy.37 = f32[8,32,4,8,1]{1,3,4,2,0:T(8,128)S(1)} copy(f32[8,32,4,8,1]{4,3,2,1,0:T(8,128)} %get-tuple-element.6) | data formatting | bytes 65536 | tf_op jit(solution)/shard_map/exp | solution.py:22
  113.3 0.2 copy.38
  113.6 2.9 %fusion.5 = f32[32,4,8,128]{3,2,1,0:T(8,128)S(1)} fusion(f32[8,32,4,8,130]{4,3,2,1,0:T(8,128)} %bitcast.16, f32[8,32,4,8]{3,2,1,0:T(4,128)S(1)} %copy.38), kind=kLoop, calls=%fused_computation.7 | loop fusion | flops 1966080 | bytes 4751360 | tf_op jit(solution)/shard_map/reduce_sum | solution.py:23
  116.5 0.9 fusion.11
  117.5 0.0 copy-done.1
Async XLA Ops:
  6.5 1.0 copy-start
  6.5 92.7 %all-gather.3.cloned.1.call-start = ((), (), s32[]{:S(2)}) async-start(), calls=%async_computation | async-start | bytes 9437184 | tf_op jit(solution)/shard_map/all_gather | solution.py:28
  24.1 1.9 %copy-start.2 = (f32[32,4,8,1024]{3,2,1,0:T(8,128)}, f32[32,4,8,1024]{3,2,1,0:T(8,128)S(1)}, u32[]{:S(2)}) copy-start(f32[32,4,8,1024]{3,2,1,0:T(8,128)S(1)} %get-tuple-element.8) | copy-start | bytes 12582916
  109.7 7.8 %copy-start.1 = (bf16[32,32,128]{2,1,0:T(8,128)(2,1)S(1)}, bf16[32,32,128]{2,1,0:T(8,128)(2,1)}, u32[]{:S(2)}) copy-start(bf16[32,32,128]{2,1,0:T(8,128)(2,1)} %param.3) | copy-start | bytes 786436
Sparse Core Ops, SparseCore 0:
  48.1 51.1 all-gather.2
where the time goes:
time: 125 us; the launch traced here: 124 us
  waiting for transfers between devices  51.3 us (41%)
  matrix products  34.6 us (28%)
  other arithmetic  16.3 us (13%)
  between operations  13.4 us (11%)
  local copies, waits for them, and re-layouts  8.56 us (7%)
    all_gather x1, waiting for transfers between devices, step(): return together(lax.all_gather(part_of(q, k, v), 'sp')).reshape(q.shape)  51.3 us
    dot_general x2, matrix products, einsum(): return jnp.einsum(form, a.astype(jnp.float32), b.astype(jnp.float32))  34.6 us
    reduce_sum x1, other arithmetic, together(): jnp.sum(total * scale, 0)  6.75 us
    exp x1, local copies, waits for them, and re-layouts, together(): scale = jnp.exp(high - jnp.max(high, 0))  3.66 us
    reduce_max x1, other arithmetic, together(): scale = jnp.exp(high - jnp.max(high, 0))  3.51 us
    reduce_sum x1, other arithmetic, together(): jnp.sum(seen * scale, 0) / jnp.sum(total * scale, 0)  2.93 us
    unnamed x6, local copies, waits for them, and re-layouts  2.87 us
  transfers between devices with their start and end apart: 1, of which 1 were waited for; matrix products, arithmetic and copies ran while one was open for 0% of the time, Pallas kernels for 0%

commit v1 on v0

v1 whole, which is shorter than its diff:
```python
import functools

import jax
import jax.numpy as jnp
from jax import lax
from jax.experimental import pallas as pl
from jax.experimental.pallas import tpu as pltpu
from jax.sharding import PartitionSpec as P

LOG2E = 1.4426950408889634
TILE = 256
TAIL = 2
LAG = 3
K_SLOTS, V_SLOTS = 4, 5


def spread(x, reduce, fill, kinds):
    lane = lax.broadcasted_iota(jnp.int32, x.shape, 1) % kinds
    out = None
    for g in range(kinds):
        one = jnp.broadcast_to(reduce(jnp.where(lane == g, x, fill), axis=1, keepdims=True), x.shape)
        out = one if out is None else jnp.where(lane == g, one, out)
    return out


def columns(x):
    return [x[:, i : i + 128] for i in range(0, x.shape[1], 128)]


def weigh(q, keys, held, scale):
    half = keys.shape[0] // 2
    none = jnp.zeros_like(q)
    both = jnp.concatenate([jnp.concatenate([q, none], 1), jnp.concatenate([none, q], 1)], 0)
    lane = lax.broadcasted_iota(jnp.int32, (8, TILE), 1) % 4
    tiles = []
    for j in range(0, half, TILE):
        pair = jnp.concatenate([keys[j : j + TILE, :], keys[half + j : half + j + TILE, :]], 1)
        scores = lax.dot_general(both, pair, (((1,), (1,)), ((), ())), preferred_element_type=jnp.float32)
        for a in (0, 32):
            own = scores[a : a + 8]
            for g in range(1, 4):
                own = jnp.where(lane == g, scores[a + 8 * g : a + 8 * g + 8], own)
            tiles.append(own)
    high = spread(functools.reduce(jnp.maximum, columns(functools.reduce(jnp.maximum, tiles))), jnp.max, -jnp.inf, 4)
    wide = jnp.concatenate([high] * (TILE // 128), 1)
    total = None
    for j in range(half // TILE):
        rows = []
        for own in tiles[2 * j : 2 * j + 2]:
            weights = jnp.exp2((own - wide) * scale)
            total = weights if total is None else total + weights
            rows += [jnp.where(lane == g, weights, 0.0) for g in range(4)]
        held[:, j * TILE : (j + 1) * TILE] = jnp.concatenate(rows, 0).astype(jnp.bfloat16)
    return high, spread(functools.reduce(jnp.add, columns(total)), jnp.sum, 0.0, 4)


def gather(held, values):
    half = values.shape[0] // 2
    out = None
    for r in range(0, half, half // 2):
        rows = jnp.concatenate([values[r : r + half // 2, :], values[half + r : half + r + half // 2, :]], 1)
        seen = jnp.dot(held[:, r : r + half // 2], rows, preferred_element_type=jnp.float32)
        seen = seen[0:32, 0:128] + seen[32:64, 128:256]
        out = seen if out is None else out + seen
    return out


def kernel(n, q, k, v, out, kbuf, vbuf, held0, held1, part, stat, parts, stats, ksem, vsem, sent, told, came, passed, landed):
    me = lax.axis_index("sp")
    pairs = q.shape[0] // 2
    bulk = pairs - TAIL
    rounds = -(-bulk // n)
    scale = q.shape[2] ** -0.5 * LOG2E
    held = (held0, held1)

    def read(src, buf, sem, slots, i):
        slot = lax.rem(i, slots)
        return pltpu.make_async_copy(src.at[pl.ds(2 * i, 2)], buf.at[slot], sem.at[slot])

    read_k = functools.partial(read, k, kbuf, ksem, K_SLOTS)
    read_v = functools.partial(read, v, vbuf, vsem, V_SLOTS)
    for i in range(max(K_SLOTS, V_SLOTS)):
        if i < K_SLOTS:
            read_k(i).start()
        if i < V_SLOTS:
            read_v(i).start()

    barrier = pltpu.get_barrier_semaphore()
    for d in range(1, n):
        pl.semaphore_signal(barrier, inc=1, device_id={"sp": lax.rem(me + d, n)}, device_id_type=pl.DeviceIdType.MESH)

    def keys(i):
        slot = lax.rem(i, K_SLOTS)
        lane = lax.broadcasted_iota(jnp.int32, (8, 128), 1)
        found = [weigh(q[2 * i + u], kbuf.at[slot, u], held[u], scale) for u in range(2)]
        stat[i] = jnp.where(lane < 64, jnp.where(lane < 32, *found[0]), jnp.where(lane < 96, *found[1]))

    def values(i):
        slot = lax.rem(i, V_SLOTS)
        for u in range(2):
            part[i, u] = gather(held[u], vbuf.at[slot, u]).astype(jnp.bfloat16)

    def send(i, place, to, sems):
        return [
            pltpu.make_async_remote_copy(
                src_ref=src.at[i], dst_ref=dst.at[place, me], send_sem=sems.at[kind], recv_sem=came.at[place, me, kind], device_id={"sp": to}, device_id_type=pl.DeviceIdType.MESH
            )
            for kind, (src, dst) in enumerate(((part, parts), (stat, stats)))
        ]

    def keep(i, place):
        parts[place, me] = part[i]
        stats[place, me] = stat[i]

    def to_owner(i):
        return send(i, i // n, lax.rem(i, n), sent.at[i])

    def to_all(i, d):
        return send(i, rounds + i - bulk, lax.rem(me + d, n), told.at[i - bulk, d - 1])

    def share(i):
        @pl.when(i < bulk)
        def _():
            @pl.when(lax.rem(i, n) == me)
            def _():
                keep(i, i // n)

            @pl.when(lax.rem(i, n) != me)
            def _():
                for copy in to_owner(i):
                    copy.start()

        @pl.when(i >= bulk)
        def _():
            for d in range(1, n):
                for copy in to_all(i, d):
                    copy.start()
            keep(i, rounds + i - bulk)

    def together(i, place):
        for d in range(1, n):
            other = lax.rem(me + d, n)
            for kind, dst in enumerate((parts, stats)):
                pltpu.make_async_remote_copy(
                    src_ref=dst.at[place, other], dst_ref=dst.at[place, other], send_sem=came.at[place, other, kind], recv_sem=came.at[place, other, kind],
                    device_id={"sp": other}, device_id_type=pl.DeviceIdType.MESH,
                ).wait_recv()
        for u in range(2):
            result = []
            for g in range(4):
                high, total = ([jnp.broadcast_to(stats[place, p][:, at : at + 1], (8, 128)) for p in range(n)] for at in (64 * u + g, 64 * u + 32 + g))
                top = functools.reduce(jnp.maximum, high)
                by = [jnp.exp2((h - top) * scale) for h in high]
                whole = functools.reduce(jnp.add, [w * t for w, t in zip(by, total)])
                seen = functools.reduce(jnp.add, [w * parts[place, p, u, 8 * g : 8 * g + 8, :].astype(jnp.float32) for p, w in enumerate(by)])
                result.append(seen / whole)
            out[2 * i + u] = jnp.concatenate(result, 0).astype(out.dtype)

    def announce(i, d):
        here = out.at[pl.ds(2 * i, 2)]
        return pltpu.make_async_remote_copy(
            src_ref=here, dst_ref=here, send_sem=passed.at[i // n, d - 1], recv_sem=landed.at[i], device_id={"sp": lax.rem(me + d, n)}, device_id_type=pl.DeviceIdType.MESH
        )

    def own(i):
        @pl.when((i >= 0) & (i < bulk) & (lax.rem(i + n, n) == me))
        def _():
            together(i, i // n)
            for d in range(1, n):
                announce(i, d).start()

    read_k(0).wait()
    keys(0)
    read_k(K_SLOTS).start()
    pl.semaphore_wait(barrier, n - 1)

    def step(i, _):
        read_v(i - 1).wait()
        read_k(i).wait()
        values(i - 1)
        keys(i)

        @pl.when(i + K_SLOTS < pairs)
        def _():
            read_k(i + K_SLOTS).start()

        @pl.when(i - 1 + V_SLOTS < pairs)
        def _():
            read_v(i - 1 + V_SLOTS).start()

        share(i - 1)
        own(i - 1 - LAG)
        return 0

    lax.fori_loop(1, pairs, step, 0)
    read_v(pairs - 1).wait()
    values(pairs - 1)
    share(jnp.int32(pairs - 1))

    def rest(i, _):
        own(i)
        return 0

    lax.fori_loop(pairs - 1 - LAG, bulk, rest, 0)

    def last(i, _):
        together(i, rounds + i - bulk)
        return 0

    lax.fori_loop(bulk, pairs, last, 0)

    def settle(i, _):
        @pl.when(lax.rem(i, n) != me)
        def _():
            announce(i, 1).wait_recv()
            for copy in to_owner(i):
                copy.wait_send()

        @pl.when(lax.rem(i, n) == me)
        def _():
            for d in range(1, n):
                announce(i, d).wait_send()

        return 0

    lax.fori_loop(0, bulk, settle, 0)
    for i in range(bulk, pairs):
        for d in range(1, n):
            for copy in to_all(i, d):
                copy.wait_send()


def solution(mesh):
    n = mesh.shape["sp"]

    def step(q, k, v):
        batch, heads, head = q.shape
        pairs, rows = batch // 2, k.shape[1] * k.shape[2]
        places = -(-(pairs - TAIL) // n) + TAIL
        dma = pltpu.SemaphoreType.DMA
        return pl.pallas_call(
            functools.partial(kernel, n),
            out_shape=jax.ShapeDtypeStruct(q.shape, q.dtype),
            in_specs=[pl.BlockSpec(memory_space=pltpu.VMEM), pl.BlockSpec(memory_space=pl.ANY), pl.BlockSpec(memory_space=pl.ANY)],
            out_specs=pl.BlockSpec(memory_space=pltpu.VMEM),
            scratch_shapes=[
                pltpu.VMEM((K_SLOTS, 2, rows, head), k.dtype),
                pltpu.VMEM((V_SLOTS, 2, rows, head), v.dtype),
                pltpu.VMEM((2 * heads, rows // 2), jnp.bfloat16),
                pltpu.VMEM((2 * heads, rows // 2), jnp.bfloat16),
                pltpu.VMEM((pairs, 2, heads, head), jnp.bfloat16),
                pltpu.VMEM((pairs, 8, 128), jnp.float32),
                pltpu.VMEM((places, n, 2, heads, head), jnp.bfloat16),
                pltpu.VMEM((places, n, 8, 128), jnp.float32),
                dma((K_SLOTS,)),
                dma((V_SLOTS,)),
                dma((pairs - TAIL, 2)),
                dma((TAIL, n - 1, 2)),
                dma((places, n, 2)),
                dma((places - TAIL, n - 1)),
                dma((pairs - TAIL,)),
            ],
            compiler_params=pltpu.CompilerParams(collective_id=0, has_side_effects=True, vmem_limit_bytes=40 * 1024 * 1024),
        )(q, k.reshape(batch, rows, head), v.reshape(batch, rows, head))

    return jax.shard_map(
        step,
        mesh=mesh,
        in_specs=(P("dp", None, None), P("dp", "sp", None, None), P("dp", "sp", None, None)),
        out_specs=P("dp", None, None),
        check_vma=False,
    )
```

time: 125 us -> 35.8 us (0.29)
  waiting for transfers between devices: 51.3 us -> 0 us
  matrix products: 34.6 us -> 0 us
  Pallas kernels: 0 us -> 34.1 us
  other arithmetic: 16.3 us -> 0 us
  between operations: 13.4 us -> 0.01 us
  local copies, waits for them, and re-layouts: 8.56 us -> 1.65 us
    all_gather x1 -> x0, waiting for transfers between devices: 51.3 us -> none  [step(): return together(lax.all_gather(part_of(q, k, v), 'sp')).reshape(q.shape)]
    dot_general x2 -> x0, matrix products: 34.6 us -> none  [einsum(): return jnp.einsum(form, a.astype(jnp.float32), b.astype(jnp.float32))]
    pallas_call x0 -> x1, Pallas kernels: none -> 34.1 us  [step(): pl.pallas_call(functools.partial(kernel, n), out_shape=jax.ShapeDtypeStru...]
    reduce_sum x3 -> x0, other arithmetic: 10.6 us -> none  [the longest x1 6.75 us: together(): jnp.sum(total * scale, 0)]
    exp x1 -> x0, local copies, waits for them, and re-layouts: 3.66 us -> none  [together(): scale = jnp.exp(high - jnp.max(high, 0))]
    reduce_max x1 -> x0, other arithmetic: 3.51 us -> none  [together(): scale = jnp.exp(high - jnp.max(high, 0))]
    broadcast_in_dim x2 -> x0, local copies, waits for them, and re-layouts: 1.63 us -> none  [the longest x1 0.82 us: part_of(): jnp.sum(weights, -1, keepdims=True)]
    concatenate x1 -> x0, other arithmetic: 1.29 us -> none  [part_of(): jnp.concatenate([seen, jnp.sum(weights, -1, keepdims=True), high], -1)]
  transfers between devices with their start and end apart: 1 -> 0, of which waited for: 1 -> 0; matrix products, arithmetic and copies ran while one was open for 0% -> 0% of each run, Pallas kernels for 0% -> 0%
where the time goes in v1:
time: 35.8 us; the launch traced here: 35.7 us
  Pallas kernels  34.1 us (95%)
  local copies, waits for them, and re-layouts  1.65 us (5%)
    pallas_call x1, Pallas kernels, step(): pl.pallas_call(functools.partial(kernel, n), out_shape=jax.ShapeDtypeStru...  34.1 us
    unnamed x3, local copies, waits for them, and re-layouts  1.65 us

profile of v1, /device:TPU:0, one launch (start us, length us, event | category | flops | bytes accessed | tf_op | source)
XLA Modules:
  0.0 35.7 jit_solution(6706708170580497291)
XLA Ops:
  0.0 0.0 copy-start
  0.0 0.9 %copy-done = bf16[32,32,128]{2,1,0:T(8,128)(2,1)S(1)} copy-done((bf16[32,32,128]{2,1,0:T(8,128)(2,1)S(1)}, bf16[32,32,128]{2,1,0:T(8,128)(2,1)}, u32[]{:S(2)}) %copy-start) | copy-done | bytes 262168
  1.0 34.1 %shard_map.37 = bf16[32,32,128]{2,1,0:T(8,128)(2,1)S(1)} custom-call(bf16[32,32,128]{2,1,0:T(8,128)(2,1)S(1)} %copy-done, bf16[32,4096,128]{2,1,0:T(8,128)(2,1)} %bitcast.2, bf16[32,4096,128]{2,1,0:T(8,128)(2,1)} %bitcast.3), custom_call_target="tpu_custom_call" | custom-call | tf_op jit(solution)/shard_map/pallas_call | solution.py:241
  35.0 0.7 %copy.5 = bf16[32,32,128]{2,1,0:T(8,128)(2,1)} copy(bf16[32,32,128]{2,1,0:T(8,128)(2,1)S(1)} %shard_map.37) | data formatting | bytes 524288
Async XLA Ops:
  0.0 0.9 %copy-start = (bf16[32,32,128]{2,1,0:T(8,128)(2,1)S(1)}, bf16[32,32,128]{2,1,0:T(8,128)(2,1)}, u32[]{:S(2)}) copy-start(bf16[32,32,128]{2,1,0:T(8,128)(2,1)} %q.1) | copy-start | bytes 786436

commit v2 on v1

--- a/solution.py
+++ b/solution.py
@@ -11,7 +11,7 @@
 TILE = 256
 TAIL = 2
 LAG = 3
-K_SLOTS, V_SLOTS = 4, 5
+K_SLOTS, V_SLOTS = 5, 6
 
 
 def spread(x, reduce, fill, kinds):
@@ -51,7 +51,7 @@
             total = weights if total is None else total + weights
             rows += [jnp.where(lane == g, weights, 0.0) for g in range(4)]
         held[:, j * TILE : (j + 1) * TILE] = jnp.concatenate(rows, 0).astype(jnp.bfloat16)
-    return high, spread(functools.reduce(jnp.add, columns(total)), jnp.sum, 0.0, 4)
+    return high, functools.reduce(jnp.add, columns(total))
 
 
 def gather(held, values):
@@ -65,7 +65,7 @@
     return out
 
 
-def kernel(n, q, k, v, out, kbuf, vbuf, held0, held1, part, stat, parts, stats, ksem, vsem, sent, told, came, passed, landed):
+def kernel(n, q, k, v, out, qbuf, kbuf, vbuf, held0, held1, high, sums, part, stat, parts, stats, qsem, ksem, vsem, sent, told, came, passed, landed):
     me = lax.axis_index("sp")
     pairs = q.shape[0] // 2
     bulk = pairs - TAIL
@@ -79,6 +79,8 @@
 
     read_k = functools.partial(read, k, kbuf, ksem, K_SLOTS)
     read_v = functools.partial(read, v, vbuf, vsem, V_SLOTS)
+    read_q = pltpu.make_async_copy(q, qbuf, qsem)
+    read_q.start()
     for i in range(max(K_SLOTS, V_SLOTS)):
         if i < K_SLOTS:
             read_k(i).start()
@@ -89,16 +91,14 @@
     for d in range(1, n):
         pl.semaphore_signal(barrier, inc=1, device_id={"sp": lax.rem(me + d, n)}, device_id_type=pl.DeviceIdType.MESH)
 
-    def keys(i):
-        slot = lax.rem(i, K_SLOTS)
+    def keys(i, u):
+        high[u], sums[u] = weigh(qbuf[2 * i + u], kbuf.at[lax.rem(i, K_SLOTS), u], held[u], scale)
+
+    def values(i, u):
         lane = lax.broadcasted_iota(jnp.int32, (8, 128), 1)
-        found = [weigh(q[2 * i + u], kbuf.at[slot, u], held[u], scale) for u in range(2)]
-        stat[i] = jnp.where(lane < 64, jnp.where(lane < 32, *found[0]), jnp.where(lane < 96, *found[1]))
-
-    def values(i):
-        slot = lax.rem(i, V_SLOTS)
-        for u in range(2):
-            part[i, u] = gather(held[u], vbuf.at[slot, u]).astype(jnp.bfloat16)
+        found = jnp.where(lane % 64 < 32, high[u], spread(sums[u], jnp.sum, 0.0, 4))
+        stat[i] = found if u == 0 else jnp.where(lane < 64, stat[i], found)
+        part[i, u] = gather(held[u], vbuf.at[lax.rem(i, V_SLOTS), u]).astype(jnp.bfloat16)
 
     def send(i, place, to, sems):
         return [
@@ -169,16 +169,22 @@
             for d in range(1, n):
                 announce(i, d).start()
 
+    read_q.wait()
     read_k(0).wait()
-    keys(0)
+    keys(0, 0)
+    keys(0, 1)
     read_k(K_SLOTS).start()
+    read_v(0).wait()
+    values(0, 0)
     pl.semaphore_wait(barrier, n - 1)
 
     def step(i, _):
-        read_v(i - 1).wait()
         read_k(i).wait()
-        values(i - 1)
-        keys(i)
+        read_v(i).wait()
+        keys(i, 0)
+        values(i - 1, 1)
+        keys(i, 1)
+        values(i, 0)
 
         @pl.when(i + K_SLOTS < pairs)
         def _():
@@ -192,16 +198,23 @@
         own(i - 1 - LAG)
         return 0
 
-    lax.fori_loop(1, pairs, step, 0)
-    read_v(pairs - 1).wait()
-    values(pairs - 1)
-    share(jnp.int32(pairs - 1))
+    end = pairs - 1
+    lax.fori_loop(1, end, step, 0)
+    read_k(end).wait()
+    keys(end, 0)
+    values(end - 1, 1)
+    share(jnp.int32(end - 1))
+    keys(end, 1)
+    read_v(end).wait()
+    values(end, 0)
+    values(end, 1)
+    share(jnp.int32(end))
 
     def rest(i, _):
         own(i)
         return 0
 
-    lax.fori_loop(pairs - 1 - LAG, bulk, rest, 0)
+    lax.fori_loop(end - 1 - LAG, bulk, rest, 0)
 
     def last(i, _):
         together(i, rounds + i - bulk)
@@ -241,17 +254,21 @@
         return pl.pallas_call(
             functools.partial(kernel, n),
             out_shape=jax.ShapeDtypeStruct(q.shape, q.dtype),
-            in_specs=[pl.BlockSpec(memory_space=pltpu.VMEM), pl.BlockSpec(memory_space=pl.ANY), pl.BlockSpec(memory_space=pl.ANY)],
+            in_specs=[pl.BlockSpec(memory_space=pltpu.HBM)] * 3,
             out_specs=pl.BlockSpec(memory_space=pltpu.VMEM),
             scratch_shapes=[
+                pltpu.VMEM(q.shape, q.dtype),
                 pltpu.VMEM((K_SLOTS, 2, rows, head), k.dtype),
                 pltpu.VMEM((V_SLOTS, 2, rows, head), v.dtype),
                 pltpu.VMEM((2 * heads, rows // 2), jnp.bfloat16),
                 pltpu.VMEM((2 * heads, rows // 2), jnp.bfloat16),
+                pltpu.VMEM((2, 8, 128), jnp.float32),
+                pltpu.VMEM((2, 8, 128), jnp.float32),
                 pltpu.VMEM((pairs, 2, heads, head), jnp.bfloat16),
                 pltpu.VMEM((pairs, 8, 128), jnp.float32),
                 pltpu.VMEM((places, n, 2, heads, head), jnp.bfloat16),
                 pltpu.VMEM((places, n, 8, 128), jnp.float32),
+                dma,
                 dma((K_SLOTS,)),
                 dma((V_SLOTS,)),
                 dma((pairs - TAIL, 2)),
@@ -260,7 +277,7 @@
                 dma((places - TAIL, n - 1)),
                 dma((pairs - TAIL,)),
             ],
-            compiler_params=pltpu.CompilerParams(collective_id=0, has_side_effects=True, vmem_limit_bytes=40 * 1024 * 1024),
+            compiler_params=pltpu.CompilerParams(collective_id=0, has_side_effects=True, vmem_limit_bytes=48 * 1024 * 1024),
         )(q, k.reshape(batch, rows, head), v.reshape(batch, rows, head))
 
     return jax.shard_map(

time: 35.8 us -> 33.3 us (0.930)
  Pallas kernels: 34.1 us -> 31.6 us
    pallas_call x1, Pallas kernels: 34.1 us -> 31.6 us  [step(): pl.pallas_call(functools.partial(kernel, n), out_shape=jax.ShapeDtypeStru...]
where the time goes in v2:
time: 33.3 us; the launch traced here: 33.2 us
  Pallas kernels  31.6 us (95%)
  local copies, waits for them, and re-layouts  1.65 us (5%)
    pallas_call x1, Pallas kernels, step(): pl.pallas_call(functools.partial(kernel, n), out_shape=jax.ShapeDtypeStru...  31.6 us
    unnamed x3, local copies, waits for them, and re-layouts  1.65 us

profile of v2, /device:TPU:0, one launch (start us, length us, event | category | flops | bytes accessed | tf_op | source)
XLA Modules:
  0.0 33.2 jit_solution(11014384431178258414)
XLA Ops:
  0.0 0.0 copy-start
  0.0 0.9 %copy-done = bf16[32,32,128]{2,1,0:T(8,128)(2,1)S(1)} copy-done((bf16[32,32,128]{2,1,0:T(8,128)(2,1)S(1)}, bf16[32,32,128]{2,1,0:T(8,128)(2,1)}, u32[]{:S(2)}) %copy-start) | copy-done | bytes 262168
  1.0 31.6 %shard_map.37 = bf16[32,32,128]{2,1,0:T(8,128)(2,1)S(1)} custom-call(bf16[32,32,128]{2,1,0:T(8,128)(2,1)S(1)} %copy-done, bf16[32,4096,128]{2,1,0:T(8,128)(2,1)} %bitcast.2, bf16[32,4096,128]{2,1,0:T(8,128)(2,1)} %bitcast.3), custom_call_target="tpu_custom_call" | custom-call | tf_op jit(solution)/shard_map/pallas_call | solution.py:254
  32.5 0.7 %copy.5 = bf16[32,32,128]{2,1,0:T(8,128)(2,1)} copy(bf16[32,32,128]{2,1,0:T(8,128)(2,1)S(1)} %shard_map.37) | data formatting | bytes 524288
Async XLA Ops:
  0.0 0.9 %copy-start = (bf16[32,32,128]{2,1,0:T(8,128)(2,1)S(1)}, bf16[32,32,128]{2,1,0:T(8,128)(2,1)}, u32[]{:S(2)}) copy-start(bf16[32,32,128]{2,1,0:T(8,128)(2,1)} %q.1) | copy-start | bytes 786436

commit v3 on v2

--- a/solution.py
+++ b/solution.py
@@ -9,9 +9,9 @@
 
 LOG2E = 1.4426950408889634
 TILE = 256
-TAIL = 2
-LAG = 3
-K_SLOTS, V_SLOTS = 5, 6
+TAIL = 3
+LAG = 4
+K_SLOTS, V_SLOTS = 4, 5
 
 
 def spread(x, reduce, fill, kinds):
@@ -65,10 +65,12 @@
     return out
 
 
-def kernel(n, q, k, v, out, qbuf, kbuf, vbuf, held0, held1, high, sums, part, stat, parts, stats, qsem, ksem, vsem, sent, told, came, passed, landed):
+def kernel(n, q, k, v, out, qbuf, kbuf, vbuf, held0, held1, high, sums, part, stat, parts, stats, qsem, ksem, vsem, sent, told, handed, came, met, passed, landed):
     me = lax.axis_index("sp")
+    mate = me + 1 - 2 * lax.rem(me, 2)
     pairs = q.shape[0] // 2
-    bulk = pairs - TAIL
+    units = pairs + 1
+    bulk = units - TAIL
     rounds = -(-bulk // n)
     scale = q.shape[2] ** -0.5 * LOG2E
     held = (held0, held1)
@@ -97,14 +99,28 @@
     def values(i, u):
         lane = lax.broadcasted_iota(jnp.int32, (8, 128), 1)
         found = jnp.where(lane % 64 < 32, high[u], spread(sums[u], jnp.sum, 0.0, 4))
-        stat[i] = found if u == 0 else jnp.where(lane < 64, stat[i], found)
-        part[i, u] = gather(held[u], vbuf.at[lax.rem(i, V_SLOTS), u]).astype(jnp.bfloat16)
-
-    def send(i, place, to, sems):
+        if u == 1:
+            stat[i + 1] = found
+        else:
+            stat[i] = jnp.where(lane < 64, stat[i], found)
+        part[i + u, 1 - u] = gather(held[u], vbuf.at[lax.rem(i, V_SLOTS), u]).astype(jnp.bfloat16)
+
+    def few(i):
+        return 1 if isinstance(i, int) and i == units - 1 else 2
+
+    def remote(src, dst, send_sem, recv_sem, to):
+        return pltpu.make_async_remote_copy(src_ref=src, dst_ref=dst, send_sem=send_sem, recv_sem=recv_sem, device_id={"sp": to}, device_id_type=pl.DeviceIdType.MESH)
+
+    def cut(ref, kind, i):
+        return ref.at[pl.ds(0, 1)] if kind == 0 and few(i) == 1 else ref
+
+    def amount(i, kind, count, sem):
+        ref = parts.at[0, pl.ds(0, count), pl.ds(0, few(i))] if kind == 0 else stats.at[0, pl.ds(0, count)]
+        return remote(ref, ref, sem, sem, mate)
+
+    def send(i, place, to, sems, arrival):
         return [
-            pltpu.make_async_remote_copy(
-                src_ref=src.at[i], dst_ref=dst.at[place, me], send_sem=sems.at[kind], recv_sem=came.at[place, me, kind], device_id={"sp": to}, device_id_type=pl.DeviceIdType.MESH
-            )
+            remote(cut(src.at[i], kind, i), cut(dst.at[place, me], kind, i), sems.at[kind], arrival.at[kind], to)
             for kind, (src, dst) in enumerate(((part, parts), (stat, stats)))
         ]
 
@@ -112,40 +128,37 @@
         parts[place, me] = part[i]
         stats[place, me] = stat[i]
 
-    def to_owner(i):
-        return send(i, i // n, lax.rem(i, n), sent.at[i])
-
-    def to_all(i, d):
-        return send(i, rounds + i - bulk, lax.rem(me + d, n), told.at[i - bulk, d - 1])
-
     def share(i):
-        @pl.when(i < bulk)
-        def _():
-            @pl.when(lax.rem(i, n) == me)
-            def _():
-                keep(i, i // n)
-
-            @pl.when(lax.rem(i, n) != me)
-            def _():
-                for copy in to_owner(i):
-                    copy.start()
-
-        @pl.when(i >= bulk)
-        def _():
-            for d in range(1, n):
-                for copy in to_all(i, d):
-                    copy.start()
-            keep(i, rounds + i - bulk)
-
-    def together(i, place):
-        for d in range(1, n):
-            other = lax.rem(me + d, n)
-            for kind, dst in enumerate((parts, stats)):
-                pltpu.make_async_remote_copy(
-                    src_ref=dst.at[place, other], dst_ref=dst.at[place, other], send_sem=came.at[place, other, kind], recv_sem=came.at[place, other, kind],
-                    device_id={"sp": other}, device_id_type=pl.DeviceIdType.MESH,
-                ).wait_recv()
-        for u in range(2):
+        @pl.when(lax.rem(i, n) == me)
+        def _():
+            keep(i, i // n)
+
+        @pl.when(lax.rem(i, n) != me)
+        def _():
+            for copy in send(i, i // n, lax.rem(i, n), sent, came.at[i // n]):
+                copy.start()
+
+    def tell(i):
+        place = rounds + i - bulk
+        for d in range(2, n, 2):
+            for copy in send(i, place, lax.rem(me + d, n), told, met.at[i - bulk, 0]):
+                copy.start()
+        for copy in send(i, place, mate, told, met.at[i - bulk, 1]):
+            copy.start()
+        keep(i, place)
+
+    def relay(i):
+        place = rounds + i - bulk
+        for kind, ref in enumerate((parts, stats)):
+            amount(i, kind, n // 2 - 1, met.at[i - bulk, 0, kind]).wait_recv()
+            for d in range(2, n, 2):
+                here = cut(ref.at[place, lax.rem(me + d, n)], kind, i)
+                remote(here, here, handed.at[kind], met.at[i - bulk, 1, kind], mate).start()
+
+    def together(i, place, arrival, count):
+        for kind in range(2):
+            amount(i, kind, count, arrival.at[kind]).wait_recv()
+        for u in range(few(i)):
             result = []
             for g in range(4):
                 high, total = ([jnp.broadcast_to(stats[place, p][:, at : at + 1], (8, 128)) for p in range(n)] for at in (64 * u + g, 64 * u + 32 + g))
@@ -156,27 +169,25 @@
                 result.append(seen / whole)
             out[2 * i + u] = jnp.concatenate(result, 0).astype(out.dtype)
 
-    def announce(i, d):
-        here = out.at[pl.ds(2 * i, 2)]
-        return pltpu.make_async_remote_copy(
-            src_ref=here, dst_ref=here, send_sem=passed.at[i // n, d - 1], recv_sem=landed.at[i], device_id={"sp": lax.rem(me + d, n)}, device_id_type=pl.DeviceIdType.MESH
-        )
-
     def own(i):
         @pl.when((i >= 0) & (i < bulk) & (lax.rem(i + n, n) == me))
         def _():
-            together(i, i // n)
+            together(i, i // n, came.at[i // n], n - 1)
+            here = out.at[pl.ds(2 * i, 2)]
             for d in range(1, n):
-                announce(i, d).start()
+                remote(here, here, passed, landed, lax.rem(me + d, n)).start()
 
     read_q.wait()
     read_k(0).wait()
+    part[0, 0] = jnp.zeros_like(part[0, 0])
+    stat[0] = jnp.ones_like(stat[0])
     keys(0, 0)
     keys(0, 1)
     read_k(K_SLOTS).start()
     read_v(0).wait()
     values(0, 0)
     pl.semaphore_wait(barrier, n - 1)
+    share(jnp.int32(0))
 
     def step(i, _):
         read_k(i).wait()
@@ -194,8 +205,15 @@
         def _():
             read_v(i - 1 + V_SLOTS).start()
 
-        share(i - 1)
-        own(i - 1 - LAG)
+        @pl.when(i < bulk)
+        def _():
+            share(i)
+
+        @pl.when(i >= bulk)
+        def _():
+            tell(i)
+
+        own(i - LAG)
         return 0
 
     end = pairs - 1
@@ -203,44 +221,48 @@
     read_k(end).wait()
     keys(end, 0)
     values(end - 1, 1)
-    share(jnp.int32(end - 1))
     keys(end, 1)
+    own(jnp.int32(end - LAG))
     read_v(end).wait()
     values(end, 0)
+    tell(end)
     values(end, 1)
-    share(jnp.int32(end))
+    tell(units - 1)
 
     def rest(i, _):
         own(i)
         return 0
 
-    lax.fori_loop(end - 1 - LAG, bulk, rest, 0)
-
-    def last(i, _):
-        together(i, rounds + i - bulk)
-        return 0
-
-    lax.fori_loop(bulk, pairs, last, 0)
-
-    def settle(i, _):
-        @pl.when(lax.rem(i, n) != me)
-        def _():
-            announce(i, 1).wait_recv()
-            for copy in to_owner(i):
-                copy.wait_send()
-
-        @pl.when(lax.rem(i, n) == me)
-        def _():
-            for d in range(1, n):
-                announce(i, d).wait_send()
-
-        return 0
-
-    lax.fori_loop(0, bulk, settle, 0)
-    for i in range(bulk, pairs):
-        for d in range(1, n):
-            for copy in to_all(i, d):
-                copy.wait_send()
+    def sequences(sem, count):
+        ref = out.at[pl.ds(0, count)]
+        remote(ref, ref, sem, sem, mate).wait_send()
+
+    def settle(mine):
+        others = pl.ds(0, bulk - mine)
+        remote(part.at[others], part.at[others], sent.at[0], landed, mate).wait()
+        remote(stat.at[others], stat.at[others], sent.at[1], landed, mate).wait_send()
+        sequences(passed, 2 * mine * (n - 1))
+
+    def finish(i):
+        together(i, rounds + i - bulk, met.at[i - bulk, 1], n // 2)
+
+    lax.fori_loop(end + 1 - LAG, bulk, rest, 0)
+    for i in range(bulk, units - 2):
+        relay(i)
+    if units - 2 > bulk:
+        finish(bulk)
+    relay(units - 2)
+    relay(units - 1)
+    for i in range(min(bulk + 1, units - 2), units - 1):
+        finish(i)
+    for sems, copies in ((told, n // 2), (handed, n // 2 - 1)):
+        sequences(sems.at[0], copies * (2 * TAIL - 1))
+        numbers = stat.at[pl.ds(0, copies * TAIL)]
+        remote(numbers, numbers, sems.at[1], sems.at[1], mate).wait_send()
+    finish(units - 1)
+    more = bulk - (rounds - 1) * n
+    pl.when(me < more)(lambda: settle(rounds))
+    pl.when(me >= more)(lambda: settle(rounds - 1))
 
 
 def solution(mesh):
@@ -248,12 +270,12 @@
 
     def step(q, k, v):
         batch, heads, head = q.shape
-        pairs, rows = batch // 2, k.shape[1] * k.shape[2]
-        places = -(-(pairs - TAIL) // n) + TAIL
+        units, rows = batch // 2 + 1, k.shape[1] * k.shape[2]
+        places = -(-(units - TAIL) // n) + TAIL
         dma = pltpu.SemaphoreType.DMA
-        return pl.pallas_call(
+        padded = pl.pallas_call(
             functools.partial(kernel, n),
-            out_shape=jax.ShapeDtypeStruct(q.shape, q.dtype),
+            out_shape=jax.ShapeDtypeStruct((2 * units, heads, head), q.dtype),
             in_specs=[pl.BlockSpec(memory_space=pltpu.HBM)] * 3,
             out_specs=pl.BlockSpec(memory_space=pltpu.VMEM),
             scratch_shapes=[
@@ -264,21 +286,24 @@
                 pltpu.VMEM((2 * heads, rows // 2), jnp.bfloat16),
                 pltpu.VMEM((2, 8, 128), jnp.float32),
                 pltpu.VMEM((2, 8, 128), jnp.float32),
-                pltpu.VMEM((pairs, 2, heads, head), jnp.bfloat16),
-                pltpu.VMEM((pairs, 8, 128), jnp.float32),
+                pltpu.VMEM((units, 2, heads, head), jnp.bfloat16),
+                pltpu.VMEM((units, 8, 128), jnp.float32),
                 pltpu.VMEM((places, n, 2, heads, head), jnp.bfloat16),
                 pltpu.VMEM((places, n, 8, 128), jnp.float32),
                 dma,
                 dma((K_SLOTS,)),
                 dma((V_SLOTS,)),
-                dma((pairs - TAIL, 2)),
-                dma((TAIL, n - 1, 2)),
-                dma((places, n, 2)),
-                dma((places - TAIL, n - 1)),
-                dma((pairs - TAIL,)),
+                dma((2,)),
+                dma((2,)),
+                dma((2,)),
+                dma((places - TAIL, 2)),
+                dma((TAIL, 2, 2)),
+                dma,
+                dma,
             ],
             compiler_params=pltpu.CompilerParams(collective_id=0, has_side_effects=True, vmem_limit_bytes=48 * 1024 * 1024),
         )(q, k.reshape(batch, rows, head), v.reshape(batch, rows, head))
+        return padded[1 : batch + 1]
 
     return jax.shard_map(
         step,

time: 33.3 us -> 31.5 us (0.946)
  Pallas kernels: 31.6 us -> 29.7 us
    pallas_call x1, Pallas kernels: 31.6 us -> 29.7 us  [step(): pl.pallas_call(functools.partial(kernel, n), out_shape=jax.ShapeDtypeStru...]
    slice x0 -> x1, local copies, waits for them, and re-layouts: none -> 0.72 us  [step(): return padded[1:batch + 1]]
    unnamed x3 -> x2, local copies, waits for them, and re-layouts: 1.65 us -> 0.95 us
where the time goes in v3:
time: 31.5 us; the launch traced here: 31.4 us
  Pallas kernels  29.7 us (94%)
  local copies, waits for them, and re-layouts  1.67 us (5%)
    pallas_call x1, Pallas kernels, step(): pl.pallas_call(functools.partial(kernel, n), out_shape=jax.ShapeDtypeStru...  29.7 us
    unnamed x2, local copies, waits for them, and re-layouts  0.95 us
    slice x1, local copies, waits for them, and re-layouts, step(): return padded[1:batch + 1]  0.72 us

profile of v3, /device:TPU:0, one launch (start us, length us, event | category | flops | bytes accessed | tf_op | source)
XLA Modules:
  0.0 31.4 jit_solution(11203384760371959292)
XLA Ops:
  0.0 0.0 copy-start
  0.0 0.9 %copy-done = bf16[32,32,128]{2,1,0:T(8,128)(2,1)S(1)} copy-done((bf16[32,32,128]{2,1,0:T(8,128)(2,1)S(1)}, bf16[32,32,128]{2,1,0:T(8,128)(2,1)}, u32[]{:S(2)}) %copy-start) | copy-done | bytes 262168
  1.0 29.7 %shard_map.37 = bf16[34,32,128]{2,1,0:T(8,128)(2,1)S(1)} custom-call(bf16[32,32,128]{2,1,0:T(8,128)(2,1)S(1)} %copy-done, bf16[32,4096,128]{2,1,0:T(8,128)(2,1)} %bitcast.2, bf16[32,4096,128]{2,1,0:T(8,128)(2,1)} %bitcast.3), custom_call_target="tpu_custom_call" | custom-call | tf_op jit(solution)/shard_map/pallas_call | solution.py:276
  30.7 0.7 %slice.3 = bf16[32,32,128]{2,1,0:T(8,128)(2,1)} slice(bf16[34,32,128]{2,1,0:T(8,128)(2,1)S(1)} %shard_map.37), slice={[1:33], [0:32], [0:128]} | slice | bytes 524288 | tf_op jit(solution)/shard_map/slice | solution.py:306
Async XLA Ops:
  0.0 0.9 %copy-start = (bf16[32,32,128]{2,1,0:T(8,128)(2,1)S(1)}, bf16[32,32,128]{2,1,0:T(8,128)(2,1)}, u32[]{:S(2)}) copy-start(bf16[32,32,128]{2,1,0:T(8,128)(2,1)} %q.1) | copy-start | bytes 786436

commit v4 on v3

--- a/solution.py
+++ b/solution.py
@@ -140,11 +140,13 @@
 
     def tell(i):
         place = rounds + i - bulk
-        for d in range(2, n, 2):
+        final = few(i) == 1
+        for d in range(1, n) if final else range(2, n, 2):
             for copy in send(i, place, lax.rem(me + d, n), told, met.at[i - bulk, 0]):
                 copy.start()
-        for copy in send(i, place, mate, told, met.at[i - bulk, 1]):
-            copy.start()
+        if not final:
+            for copy in send(i, place, mate, told, met.at[i - bulk, 1]):
+                copy.start()
         keep(i, place)
 
     def relay(i):
@@ -252,14 +254,13 @@
     if units - 2 > bulk:
         finish(bulk)
     relay(units - 2)
-    relay(units - 1)
     for i in range(min(bulk + 1, units - 2), units - 1):
         finish(i)
-    for sems, copies in ((told, n // 2), (handed, n // 2 - 1)):
-        sequences(sems.at[0], copies * (2 * TAIL - 1))
-        numbers = stat.at[pl.ds(0, copies * TAIL)]
+    for sems, copies, more in ((told, n // 2, n - 1), (handed, n // 2 - 1, 0)):
+        sequences(sems.at[0], copies * (2 * TAIL - 2) + more)
+        numbers = stat.at[pl.ds(0, copies * (TAIL - 1) + more)]
         remote(numbers, numbers, sems.at[1], sems.at[1], mate).wait_send()
-    finish(units - 1)
+    together(units - 1, rounds + TAIL - 1, met.at[TAIL - 1, 0], n - 1)
     more = bulk - (rounds - 1) * n
     pl.when(me < more)(lambda: settle(rounds))
     pl.when(me >= more)(lambda: settle(rounds - 1))
@@ -302,7 +303,7 @@
                 dma,
             ],
             compiler_params=pltpu.CompilerParams(collective_id=0, has_side_effects=True, vmem_limit_bytes=48 * 1024 * 1024),
-        )(q, k.reshape(batch, rows, head), v.reshape(batch, rows, head))
+        )(pltpu.with_memory_space_constraint(q, pltpu.HBM), k.reshape(batch, rows, head), v.reshape(batch, rows, head))
         return padded[1 : batch + 1]
 
     return jax.shard_map(

time: 31.5 us -> 33 us (1.048)
  Pallas kernels: 29.7 us -> 32.2 us
  local copies, waits for them, and re-layouts: 1.67 us -> 0.72 us
    pallas_call x1, Pallas kernels: 29.7 us -> 32.2 us  [step(): pl.pallas_call(functools.partial(kernel, n), out_shape=jax.ShapeDtypeStru...]
    unnamed x2 -> x0, local copies, waits for them, and re-layouts: 0.95 us -> none
where the time goes in v4:
time: 33 us; the launch traced here: 32.9 us
  Pallas kernels  32.2 us (98%)
  local copies, waits for them, and re-layouts  0.72 us (2%)
    pallas_call x1, Pallas kernels, step(): pl.pallas_call(functools.partial(kernel, n), out_shape=jax.ShapeDtypeStru...  32.2 us
    slice x1, local copies, waits for them, and re-layouts, step(): return padded[1:batch + 1]  0.72 us

profile of v4, /device:TPU:0, one launch (start us, length us, event | category | flops | bytes accessed | tf_op | source)
XLA Modules:
  0.0 32.9 jit_solution(8097476819795589357)
XLA Ops:
  0.0 32.2 %shard_map.37 = bf16[34,32,128]{2,1,0:T(8,128)(2,1)S(1)} custom-call(bf16[32,32,128]{2,1,0:T(8,128)(2,1)} %q.1, bf16[32,4096,128]{2,1,0:T(8,128)(2,1)} %bitcast.2, bf16[32,4096,128]{2,1,0:T(8,128)(2,1)} %bitcast.3), custom_call_target="tpu_custom_call" | custom-call | tf_op jit(solution)/shard_map/pallas_call | solution.py:277
  32.2 0.7 %slice.3 = bf16[32,32,128]{2,1,0:T(8,128)(2,1)} slice(bf16[34,32,128]{2,1,0:T(8,128)(2,1)S(1)} %shard_map.37), slice={[1:33], [0:32], [0:128]} | slice | bytes 524288 | tf_op jit(solution)/shard_map/slice | solution.py:307

commit v5 on v4

--- a/solution.py
+++ b/solution.py
@@ -11,7 +11,7 @@
 TILE = 256
 TAIL = 3
 LAG = 4
-K_SLOTS, V_SLOTS = 4, 5
+K_SLOTS, V_SLOTS = 3, 4
 
 
 def spread(x, reduce, fill, kinds):
@@ -83,11 +83,8 @@
     read_v = functools.partial(read, v, vbuf, vsem, V_SLOTS)
     read_q = pltpu.make_async_copy(q, qbuf, qsem)
     read_q.start()
-    for i in range(max(K_SLOTS, V_SLOTS)):
-        if i < K_SLOTS:
-            read_k(i).start()
-        if i < V_SLOTS:
-            read_v(i).start()
+    read_k(0).start()
+    read_v(0).start()
 
     barrier = pltpu.get_barrier_semaphore()
     for d in range(1, n):
@@ -180,11 +177,20 @@
                 remote(here, here, passed, landed, lax.rem(me + d, n)).start()
 
     read_q.wait()
+    read_k(1).start()
+    read_v(1).start()
     read_k(0).wait()
+    read_k(2).start()
+    read_v(2).start()
     part[0, 0] = jnp.zeros_like(part[0, 0])
     stat[0] = jnp.ones_like(stat[0])
     keys(0, 0)
     keys(0, 1)
+    for i in range(3, max(K_SLOTS, V_SLOTS)):
+        if i < K_SLOTS:
+            read_k(i).start()
+        if i < V_SLOTS:
+            read_v(i).start()
     read_k(K_SLOTS).start()
     read_v(0).wait()
     values(0, 0)

time: 33 us -> 30.5 us (0.924)
  Pallas kernels: 32.2 us -> 29.7 us
    pallas_call x1, Pallas kernels: 32.2 us -> 29.7 us  [step(): pl.pallas_call(functools.partial(kernel, n), out_shape=jax.ShapeDtypeStru...]
where the time goes in v5:
time: 30.5 us; the launch traced here: 30.4 us
  Pallas kernels  29.7 us (97%)
  local copies, waits for them, and re-layouts  0.72 us (2%)
    pallas_call x1, Pallas kernels, step(): pl.pallas_call(functools.partial(kernel, n), out_shape=jax.ShapeDtypeStru...  29.7 us
    slice x1, local copies, waits for them, and re-layouts, step(): return padded[1:batch + 1]  0.72 us

profile of v5, /device:TPU:0, one launch (start us, length us, event | category | flops | bytes accessed | tf_op | source)
XLA Modules:
  0.0 30.4 jit_solution(15490381259444707648)
XLA Ops:
  0.0 29.7 %shard_map.37 = bf16[34,32,128]{2,1,0:T(8,128)(2,1)S(1)} custom-call(bf16[32,32,128]{2,1,0:T(8,128)(2,1)} %q.1, bf16[32,4096,128]{2,1,0:T(8,128)(2,1)} %bitcast.2, bf16[32,4096,128]{2,1,0:T(8,128)(2,1)} %bitcast.3), custom_call_target="tpu_custom_call" | custom-call | tf_op jit(solution)/shard_map/pallas_call | solution.py:283
  29.7 0.7 %slice.3 = bf16[32,32,128]{2,1,0:T(8,128)(2,1)} slice(bf16[34,32,128]{2,1,0:T(8,128)(2,1)S(1)} %shard_map.37), slice={[1:33], [0:32], [0:128]} | slice | bytes 524288 | tf_op jit(solution)/shard_map/slice | solution.py:313

commit v6 on v5

--- a/solution.py
+++ b/solution.py
@@ -9,7 +9,7 @@
 
 LOG2E = 1.4426950408889634
 TILE = 256
-TAIL = 3
+TAIL = 2
 LAG = 4
 K_SLOTS, V_SLOTS = 3, 4
 

time: 30.5 us -> 30.3 us (level)
  no operation moved by 1% of the time
where the time goes in v6:
time: 30.3 us
  Pallas kernels  29.5 us (97%)
  local copies, waits for them, and re-layouts  0.72 us (2%)
    pallas_call x1, Pallas kernels, step(): pl.pallas_call(functools.partial(kernel, n), out_shape=jax.ShapeDtypeStru...  29.5 us
    slice x1, local copies, waits for them, and re-layouts, step(): return padded[1:batch + 1]  0.72 us

profile of v6, /device:TPU:0, one launch (start us, length us, event | category | flops | bytes accessed | tf_op | source)
XLA Modules:
  0.0 30.3 jit_solution(7467523669061925076)
XLA Ops:
  0.0 29.5 %shard_map.37 = bf16[34,32,128]{2,1,0:T(8,128)(2,1)S(1)} custom-call(bf16[32,32,128]{2,1,0:T(8,128)(2,1)} %q.1, bf16[32,4096,128]{2,1,0:T(8,128)(2,1)} %bitcast.2, bf16[32,4096,128]{2,1,0:T(8,128)(2,1)} %bitcast.3), custom_call_target="tpu_custom_call" | custom-call | tf_op jit(solution)/shard_map/pallas_call | solution.py:283
  29.5 0.7 %slice.3 = bf16[32,32,128]{2,1,0:T(8,128)(2,1)} slice(bf16[34,32,128]{2,1,0:T(8,128)(2,1)S(1)} %shard_map.37), slice={[1:33], [0:32], [0:128]} | slice | bytes 524288 | tf_op jit(solution)/shard_map/slice | solution.py:313

commit v7 on v6

--- a/solution.py
+++ b/solution.py
@@ -203,15 +203,9 @@
         keys(i, 0)
         values(i - 1, 1)
         keys(i, 1)
+        pl.when(i + K_SLOTS < pairs)(lambda: read_k(i + K_SLOTS).start())
+        pl.when(i - 1 + V_SLOTS < pairs)(lambda: read_v(i - 1 + V_SLOTS).start())
         values(i, 0)
-
-        @pl.when(i + K_SLOTS < pairs)
-        def _():
-            read_k(i + K_SLOTS).start()
-
-        @pl.when(i - 1 + V_SLOTS < pairs)
-        def _():
-            read_v(i - 1 + V_SLOTS).start()
 
         @pl.when(i < bulk)
         def _():

time: 30.3 us -> 30.3 us (level)
  no operation moved by 1% of the time
where the time goes in v7:
time: 30.3 us
  Pallas kernels  29.5 us (97%)
  local copies, waits for them, and re-layouts  0.72 us (2%)
    pallas_call x1, Pallas kernels, step(): pl.pallas_call(functools.partial(kernel, n), out_shape=jax.ShapeDtypeStru...  29.5 us
    slice x1, local copies, waits for them, and re-layouts, step(): return padded[1:batch + 1]  0.72 us

profile of v7, /device:TPU:0, one launch (start us, length us, event | category | flops | bytes accessed | tf_op | source)
XLA Modules:
  0.0 30.3 jit_solution(16220516016096832114)
XLA Ops:
  0.0 29.5 %shard_map.37 = bf16[34,32,128]{2,1,0:T(8,128)(2,1)S(1)} custom-call(bf16[32,32,128]{2,1,0:T(8,128)(2,1)} %q.1, bf16[32,4096,128]{2,1,0:T(8,128)(2,1)} %bitcast.2, bf16[32,4096,128]{2,1,0:T(8,128)(2,1)} %bitcast.3), custom_call_target="tpu_custom_call" | custom-call | tf_op jit(solution)/shard_map/pallas_call | solution.py:277
  29.5 0.7 %slice.3 = bf16[32,32,128]{2,1,0:T(8,128)(2,1)} slice(bf16[34,32,128]{2,1,0:T(8,128)(2,1)S(1)} %shard_map.37), slice={[1:33], [0:32], [0:128]} | slice | bytes 524288 | tf_op jit(solution)/shard_map/slice | solution.py:307
